TPU v7x, 32 devices: a whole 2x2x4 slice. The times are simulated.
32 devices in a mesh: wide: 8 (over z, core), narrow: 4 (over y, x).
Axes of the slice: x: 2, y: 2, z: 4, core: 2. Of those that a mesh axis runs over, the one named last changes fastest.
Arguments:
- tridiag_vectors: float32 [128, 131072], P(('wide', 'narrow')), may hold values from -6 to 6
- reflectors: float32 [2, 131072, 256], P(None, 'wide'), may hold values from -0.015625 to 0.015625
- triangles: float32 [2, 256, 256], replicated, as said below
- lower_blocks: float32 [6, 1536, 1536], P(None, 'wide'), may hold values from -0.109375 to 0.109375
- diag_inverses: float32 [4, 1536, 1536], P(None, None, 'wide'), as said below
Outputs:
- transformed: float32 [128, 131072], P('narrow', 'wide')
- solved: float32 [128, 4, 1536], P('narrow', None, 'wide')
Inputs may be any that keep to these rules, and one draw needn't show every extreme that they name: `triangles`: zero below the diagonal, positive on it. `diag_inverses`: zero above the diagonal, positive on it.
All inputs are finite; a program needn't handle non-finite values.
Results may differ from a plain program's by a relative error of at most 0.00019.
Values sent between devices are 32-bit elements; how exact they have to be, the bound alone decides.
A program may use at most 128 MiB of HBM per device.

v0:
```python
import jax
import jax.numpy as jnp
from jax import lax
from jax.sharding import PartitionSpec as P

HIGHEST = lax.Precision.HIGHEST


def reflect(current, vectors, factor, products):
    coeffs = jnp.dot(products, factor.T, precision=HIGHEST)
    return current - jnp.dot(coeffs, vectors.T, precision=HIGHEST)


def add_piece(inverse, segment):
    return jnp.dot(segment, inverse, precision=HIGHEST)


def solve_chain(corner, lower_blocks, diag_inverses):
    local_count, panels, share_cols = corner.shape
    zeroed = jnp.zeros((local_count, share_cols), jnp.float32)
    pending = [zeroed] * panels
    results = [zeroed] * panels
    for source in reversed(range(panels)):
        remain = corner[:, source, :] - pending[source]
        solution = add_piece(
            diag_inverses[source], lax.all_gather(remain, "wide", axis=1, tiled=True)
        )
        results[source] = solution
        if source > 0:
            offset = source * (source - 1) // 2
            blocks = lower_blocks[offset : offset + source]
            partial_terms = jnp.einsum("ks,qsc->kqc", solution, blocks, precision=HIGHEST)
            scattered = lax.psum_scatter(partial_terms, "wide", scatter_dimension=2, tiled=True)
            for target in range(source):
                pending[target] = pending[target] + scattered[:, target, :]
    return jnp.stack(results, axis=1)


def body(tridiag_vectors, reflectors, triangles, lower_blocks, diag_inverses):
    wide_size = lax.axis_size("wide")
    spread = lax.all_to_all(
        tridiag_vectors, ("wide", "narrow"), split_axis=1, concat_axis=0, tiled=True
    )
    current = lax.all_to_all(spread, "narrow", split_axis=0, concat_axis=1, tiled=True)
    for which in (1, 0):
        products = lax.psum(jnp.dot(current, reflectors[which], precision=HIGHEST), "wide")
        current = reflect(current, reflectors[which], triangles[which], products)
    panels, panel_rows, share_cols = diag_inverses.shape
    corner_span = panels * panel_rows
    tail_cols = current[:, current.shape[1] - corner_span :]
    framed = tail_cols.reshape(tail_cols.shape[0], panels, wide_size, share_cols)
    received = lax.all_to_all(framed, "wide", split_axis=2, concat_axis=2, tiled=True)
    corner = received[:, :, wide_size - 1, :]
    solved = solve_chain(corner, lower_blocks, diag_inverses)
    return (current, solved)


def solution(mesh):
    placed = (
        P(("wide", "narrow"), None),
        P(None, "wide", None),
        P(),
        P(None, "wide", None),
        P(None, None, "wide"),
    )
    return jax.shard_map(
        body,
        mesh=mesh,
        in_specs=placed,
        out_specs=(P("narrow", "wide"), P("narrow", None, "wide")),
        check_vma=False,
    )
```

profile of v0, /device:TPU:0, one launch (start us, length us, event | category | flops | bytes accessed | tf_op | source)
XLA Modules:
  0.0 433.0 jit_solution(8765695923981802089)
XLA Ops:
  7.2 56.5 %all_to_all.40 = f32[4,32,4096]{2,0,1:T(4,128)} all-to-all(f32[4,32,4096]{2,0,1:T(4,128)} %bitcast.93), channel_id=1, replica_groups=mesh['wide'=8,'narrow'=4] {'wide','narrow'}, dimensions={1} | all-to-all | bytes 4194304 | tf_op jit(solution)/shard_map/all_to_all | solution.py:41
  63.7 2.0 all_to_all.32
  65.6 28.2 %all_to_all.41 = f32[4,32,4096]{2,1,0:T(8,128)S(1)} all-to-all(f32[4,32,4096]{2,1,0:T(8,128)S(1)} %all_to_all.32), channel_id=1, replica_groups=mesh['wide'=8,'narrow'=4] {'narrow'}, dimensions={0} | all-to-all | bytes 4194304 | tf_op jit(solution)/shard_map/all_to_all | solution.py:44
  93.8 0.1 copy.39
  94.0 1.3 copy-done
  95.3 10.7 %fusion.4 = f32[32,256]{1,0:T(8,128)S(1)} fusion(f32[32,16384]{1,0:T(8,128)S(1)} %bitcast.83, f32[2,16384,256]{2,1,0:T(8,128)} %param.6), kind=kOutput, calls=%fused_computation.6 | convolution fusion | flops 1610612736 | bytes 18907136 | tf_op jit(solution)/shard_map/dot_general | solution.py:46
  106.0 26.1 %psum.14 = f32[32,256]{1,0:T(8,128)S(1)} all-reduce(f32[32,256]{1,0:T(8,128)S(1)} %fusion.4), channel_id=1, replica_groups=mesh['wide'=8,'narrow'=4] {'wide'}, use_global_device_ids=true, to_apply=%region_0.0 | all-reduce | flops 8192 | bytes 65536 | tf_op jit(solution)/shard_map/psum | solution.py:46
  132.1 0.3 fusion.33
  132.5 18.6 %convolution_subtract_fusion.1 = f32[32,16384]{1,0:T(8,128)S(1)} fusion(f32[32,16384]{1,0:T(8,128)} %bitcast.84, f32[32,256]{1,0:T(8,128)S(1)} %fusion.33, f32[2,16384,256]{2,1,0:T(8,128)} %param.6), kind=kOutput, calls=%fused_computation.1 | convolution fusion | flops 1611137024 | bytes 21004288 | tf_op jit(solution)/shard_map/dot_general | solution.py:11
  151.1 10.6 %fusion.1 = f32[32,256]{1,0:T(8,128)S(1)} fusion(f32[32,16384]{1,0:T(8,128)S(1)} %convolution_subtract_fusion.1, f32[2,16384,256]{2,1,0:T(8,128)} %param.6), kind=kOutput, calls=%fused_computation.3 | convolution fusion | flops 1610612736 | bytes 18907136 | tf_op jit(solution)/shard_map/dot_general | solution.py:46
  161.8 26.2 %psum.15 = f32[32,256]{1,0:T(8,128)S(1)} all-reduce(f32[32,256]{1,0:T(8,128)S(1)} %fusion.1), channel_id=1, replica_groups=mesh['wide'=8,'narrow'=4] {'wide'}, use_global_device_ids=true, to_apply=%region_1.0 | all-reduce | flops 8192 | bytes 65536 | tf_op jit(solution)/shard_map/psum | solution.py:46
  187.9 0.3 fusion.31
  188.3 17.3 %convolution_subtract_fusion = f32[32,16384]{1,0:T(8,128)S(1)} fusion(f32[32,16384]{1,0:T(8,128)S(1)} %convolution_subtract_fusion.1, f32[32,256]{1,0:T(8,128)S(1)} %fusion.31, f32[2,16384,256]{2,1,0:T(8,128)} %param.6), kind=kOutput, calls=%fused_computation | convolution fusion | flops 1611137024 | bytes 21004288 | tf_op jit(solution)/shard_map/dot_general | solution.py:11
  205.5 1.3 copy-done.1
  206.9 0.5 reshape.24
  207.4 0.6 copy.22
  208.0 29.0 %all_to_all.42 = f32[32,4,8,192]{3,0,1,2:T(8,128)S(1)} all-to-all(f32[32,4,8,192]{3,0,1,2:T(8,128)S(1)} %copy.22), channel_id=1, replica_groups=mesh['wide'=8,'narrow'=4] {'wide'}, dimensions={2} | all-to-all | bytes 1572864 | tf_op jit(solution)/shard_map/all_to_all | solution.py:52
  237.0 0.1 copy.23
  237.1 15.7 %all-gather = f32[32,1,1536]{0,1,2:T(1,128)S(1)} all-gather(f32[32,1,192]{0,1,2:T(1,128)S(1)} %copy.23), channel_id=2, replica_groups=mesh['wide'=8,'narrow'=4] {'wide'}, dimensions={2}, use_global_device_ids=true | all-gather | bytes 221184 | tf_op jit(solution)/shard_map/all_gather | solution.py:26
  252.9 2.6 fusion.21
  255.5 5.0 %fusion.10 = f32[32,3,1536]{2,0,1:T(8,128)} fusion(f32[6,192,1536]{2,1,0:T(8,128)} %param.8, f32[32,192]{1,0:T(8,128)S(1)} %fusion.21), kind=kOutput, calls=%fused_computation.12 | convolution fusion | flops 339738624 | bytes 4153344 | tf_op jit(solution)/shard_map/ks,qsc->kqc/dot_general | solution.py:32
  260.5 2.6 copy.28
  263.2 2.2 reshape.32
  265.5 29.5 %reduce-scatter.10.cloned.1.call-done = f32[192,96]{1,0:T(8,128)} async-done(((f32[1536,96]{1,0:T(8,128)}), f32[192,96]{1,0:T(8,128)}) %reduce-scatter.10.cloned.1.call-update) | async-done | bytes 73744
  295.0 1.1 reshape.33
  296.1 0.2 fusion.39
  296.3 0.1 copy.35
  296.4 0.1 copy.24
  296.5 16.0 %all-gather.1 = f32[32,1,1536]{0,1,2:T(1,128)S(1)} all-gather(f32[32,1,192]{0,1,2:T(1,128)S(1)} %copy.24), channel_id=3, replica_groups=mesh['wide'=8,'narrow'=4] {'wide'}, dimensions={2}, use_global_device_ids=true | all-gather | bytes 221184 | tf_op jit(solution)/shard_map/all_gather | solution.py:26
  312.5 2.6 fusion.19
  315.1 3.2 fusion.12
  318.3 0.8 copy.30
  319.1 1.8 reshape.34
  321.0 0.1 copy.37
  321.0 30.2 %reduce-scatter.12.cloned.1.call-done = f32[192,64]{1,0:T(8,128)} async-done(((f32[1536,64]{1,0:T(8,128)}), f32[192,64]{1,0:T(8,128)}) %reduce-scatter.12.cloned.1.call-update) | async-done | bytes 49168
  351.2 1.0 reshape.35
  352.3 0.2 fusion.40
  352.5 0.1 copy.25
  352.6 15.7 %all-gather.2 = f32[32,1,1536]{0,1,2:T(1,128)S(1)} all-gather(f32[32,1,192]{0,1,2:T(1,128)S(1)} %copy.25), channel_id=4, replica_groups=mesh['wide'=8,'narrow'=4] {'wide'}, dimensions={2}, use_global_device_ids=true | all-gather | bytes 221184 | tf_op jit(solution)/shard_map/all_gather | solution.py:26
  368.4 2.6 fusion.17
  371.0 4.8 %convolution_bitcast_fusion = f32[1536,32]{1,0:T(8,128)} fusion(f32[32,192]{1,0:T(8,128)S(1)} %fusion.17, f32[6,192,1536]{2,1,0:T(8,128)} %param.8), kind=kOutput, calls=%fused_computation.14 | convolution fusion | flops 113246208 | bytes 1400832 | tf_op jit(solution)/shard_map/ks,qsc->kqc/dot_general | solution.py:32
  375.9 0.1 copy.36
  375.9 30.3 %reduce-scatter.14.cloned.1.call-done = f32[192,32]{1,0:T(8,128)} async-done(((f32[1536,32]{1,0:T(8,128)}), f32[192,32]{1,0:T(8,128)}) %reduce-scatter.14.cloned.1.call-update) | async-done | bytes 24592
  406.3 1.0 copy.33
  407.2 0.1 copy.26
  407.3 15.7 %all-gather.3 = f32[32,1,1536]{0,1,2:T(1,128)S(1)} all-gather(f32[32,1,192]{0,1,2:T(1,128)S(1)} %copy.26), channel_id=5, replica_groups=mesh['wide'=8,'narrow'=4] {'wide'}, dimensions={2}, use_global_device_ids=true | all-gather | bytes 221184 | tf_op jit(solution)/shard_map/all_gather | solution.py:26
  423.1 2.6 fusion.28
  425.7 0.7 copy.27
  (19 shorter events, 0.4 us)
Async XLA Ops:
  7.2 287.9 %reduce-scatter.10.cloned.1.call-start = ((), (), s32[]{:S(2)}) async-start(), calls=%async_computation.6 | async-start | bytes 884736
  94.0 1.3 copy-start
  95.3 36.8 %copy-start.2 = (f32[2,256,256]{2,1,0:T(8,128)S(1)}, f32[2,256,256]{2,1,0:T(8,128)}, u32[]{:S(2)}) copy-start(f32[2,256,256]{2,1,0:T(8,128)} %param.7) | copy-start | bytes 1572868
  205.5 1.3 copy-start.1
  265.4 85.8 %reduce-scatter.12.cloned.1.call-start = ((), (), s32[]{:S(2)}) async-start(), calls=%async_computation.7 | async-start | bytes 884736
  320.9 85.4 %reduce-scatter.14.cloned.1.call-start = ((), (), s32[]{:S(2)}) async-start(), calls=%async_computation.8 | async-start | bytes 884736
Sparse Core Ops, SparseCore 0:
  265.6 29.4 reduce-scatter.9
  321.0 30.1 reduce-scatter.11
  375.9 30.2 reduce-scatter.13
where the time goes:
time: 434 us; the launch traced here: 433 us
  blocking collectives  229 us (53%)
  waiting for transfers between devices  90.1 us (21%)
  matrix products  81.5 us (19%)
  local copies, waits for them, and re-layouts  18.2 us (4%)
  between operations  14 us (3%)
    unnamed x6, waiting for transfers between devices  90.1 us
    all_gather x4, blocking collectives, solve_chain(): lax.all_gather(remain, 'wide', axis=1, tiled=True)  63.2 us
    all_to_all x1, blocking collectives, body(): lax.all_to_all(tridiag_vectors, ('wide', 'narrow'), split_axis=1, concat_...  56.5 us
    psum x2, blocking collectives, body(): lax.psum(jnp.dot(current, reflectors[which], precision=HIGHEST), 'wide')  52.3 us
    dot_general x2, matrix products, reflect(): return current - jnp.dot(coeffs, vectors.T, precision=HIGHEST)  35.9 us
    all_to_all x1, blocking collectives, body(): lax.all_to_all(framed, 'wide', split_axis=2, concat_axis=2, tiled=True)  29 us
    all_to_all x1, blocking collectives, body(): lax.all_to_all(spread, 'narrow', split_axis=0, concat_axis=1, tiled=True)  28.2 us
    dot_general x2, matrix products, body(): jnp.dot(current, reflectors[which], precision=HIGHEST)  21.3 us
  transfers between devices with their start and end apart: 3, of which 3 were waited for; matrix products, arithmetic and copies ran while one was open for 0% of the time, Pallas kernels for 0%

commit v1 on v0

--- a/solution.py
+++ b/solution.py
@@ -43,7 +43,8 @@
     )
     current = lax.all_to_all(spread, "narrow", split_axis=0, concat_axis=1, tiled=True)
     for which in (1, 0):
-        products = lax.psum(jnp.dot(current, reflectors[which], precision=HIGHEST), "wide")
+        face_match = lambda field: jnp.sum(lax.all_gather(field, "wide"), axis=0)
+        products = face_match(jnp.dot(current, reflectors[which], precision=HIGHEST))
         current = reflect(current, reflectors[which], triangles[which], products)
     panels, panel_rows, share_cols = diag_inverses.shape
     corner_span = panels * panel_rows

time: 434 us -> 410 us (0.945)
  blocking collectives: 229 us -> 206 us
    psum x2 -> x0, blocking collectives: 52.3 us -> none  [body(): lax.psum(jnp.dot(current, reflectors[which], precision=HIGHEST), 'wide')]
    all_gather x0 -> x2, blocking collectives: none -> 28.8 us  [body(): face_match = lambda field: jnp.sum(lax.all_gather(field, 'wide'), axis=0)]
where the time goes in v1:
time: 410 us
  blocking collectives  206 us (50%)
  waiting for transfers between devices  89.9 us (22%)
  matrix products  82.2 us (20%)
  local copies, waits for them, and re-layouts  16.9 us (4%)
  between operations  14 us (3%)
    unnamed x6, waiting for transfers between devices  89.9 us
    all_gather x4, blocking collectives, solve_chain(): lax.all_gather(remain, 'wide', axis=1, tiled=True)  63.2 us
    all_to_all x1, blocking collectives, body(): lax.all_to_all(tridiag_vectors, ('wide', 'narrow'), split_axis=1, concat_...  56.5 us
    dot_general x2, matrix products, reflect(): return current - jnp.dot(coeffs, vectors.T, precision=HIGHEST)  35.9 us
    all_to_all x1, blocking collectives, body(): lax.all_to_all(framed, 'wide', split_axis=2, concat_axis=2, tiled=True)  29.7 us
    all_gather x2, blocking collectives, body(): face_match = lambda field: jnp.sum(lax.all_gather(field, 'wide'), axis=0)  28.8 us
    all_to_all x1, blocking collectives, body(): lax.all_to_all(spread, 'narrow', split_axis=0, concat_axis=1, tiled=True)  28.2 us
    dot_general x2, matrix products, body(): jnp.dot(current, reflectors[which], precision=HIGHEST)  22.1 us
  transfers between devices with their start and end apart: 3, of which 3 were waited for; matrix products, arithmetic and copies ran while one was open for 0% of the time, Pallas kernels for 0%

profile of v1, /device:TPU:0, one launch (start us, length us, event | category | flops | bytes accessed | tf_op | source)
XLA Modules:
  0.0 409.5 jit_solution(6941237816644006626)
XLA Ops:
  7.2 56.5 %all_to_all.40 = f32[4,32,4096]{2,0,1:T(4,128)} all-to-all(f32[4,32,4096]{2,0,1:T(4,128)} %bitcast.95), channel_id=1, replica_groups=mesh['wide'=8,'narrow'=4] {'wide','narrow'}, dimensions={1} | all-to-all | bytes 4194304 | tf_op jit(solution)/shard_map/all_to_all | solution.py:41
  63.7 2.0 all_to_all.32
  65.6 28.2 %all_to_all.41 = f32[4,32,4096]{2,1,0:T(8,128)S(1)} all-to-all(f32[4,32,4096]{2,1,0:T(8,128)S(1)} %all_to_all.32), channel_id=1, replica_groups=mesh['wide'=8,'narrow'=4] {'narrow'}, dimensions={0} | all-to-all | bytes 4194304 | tf_op jit(solution)/shard_map/all_to_all | solution.py:44
  93.8 0.1 copy.39
  94.0 11.4 %fusion.4 = f32[32,256]{1,0:T(8,128)S(1)} fusion(f32[32,16384]{1,0:T(8,128)S(1)} %bitcast.85, f32[2,16384,256]{2,1,0:T(8,128)} %param.6), kind=kOutput, calls=%fused_computation.6 | convolution fusion | flops 1610612736 | bytes 18907136 | tf_op jit(solution)/shard_map/dot_general | solution.py:47
  105.4 14.4 %all-gather = f32[256,256]{1,0:T(8,128)S(1)} all-gather(f32[32,256]{1,0:T(8,128)S(1)} %fusion.4), channel_id=2, replica_groups=mesh['wide'=8,'narrow'=4] {'wide'}, dimensions={0}, use_global_device_ids=true | all-gather | bytes 294912 | tf_op jit(solution)/shard_map/all_gather | solution.py:46
  119.8 0.3 fusion.33
  120.2 18.6 %convolution_subtract_fusion.1 = f32[32,16384]{1,0:T(8,128)S(1)} fusion(f32[32,16384]{1,0:T(8,128)} %bitcast.86, f32[32,256]{1,0:T(8,128)S(1)} %fusion.33, f32[2,16384,256]{2,1,0:T(8,128)} %param.6), kind=kOutput, calls=%fused_computation.1 | convolution fusion | flops 1611137024 | bytes 21004288 | tf_op jit(solution)/shard_map/dot_general | solution.py:11
  138.8 10.7 %fusion.1 = f32[32,256]{1,0:T(8,128)S(1)} fusion(f32[32,16384]{1,0:T(8,128)S(1)} %convolution_subtract_fusion.1, f32[2,16384,256]{2,1,0:T(8,128)} %param.6), kind=kOutput, calls=%fused_computation.3 | convolution fusion | flops 1610612736 | bytes 18907136 | tf_op jit(solution)/shard_map/dot_general | solution.py:47
  149.5 14.4 %all-gather.1 = f32[256,256]{1,0:T(8,128)S(1)} all-gather(f32[32,256]{1,0:T(8,128)S(1)} %fusion.1), channel_id=3, replica_groups=mesh['wide'=8,'narrow'=4] {'wide'}, dimensions={0}, use_global_device_ids=true | all-gather | bytes 294912 | tf_op jit(solution)/shard_map/all_gather | solution.py:46
  163.9 0.3 fusion.31
  164.2 17.3 %convolution_subtract_fusion = f32[32,16384]{1,0:T(8,128)S(1)} fusion(f32[32,16384]{1,0:T(8,128)S(1)} %convolution_subtract_fusion.1, f32[32,256]{1,0:T(8,128)S(1)} %fusion.31, f32[2,16384,256]{2,1,0:T(8,128)} %param.6), kind=kOutput, calls=%fused_computation | convolution fusion | flops 1611137024 | bytes 21004288 | tf_op jit(solution)/shard_map/dot_general | solution.py:11
  181.5 1.3 copy-done.1
  182.9 0.5 reshape.24
  183.4 0.6 copy.22
  184.0 29.7 %all_to_all.42 = f32[32,4,8,192]{3,0,1,2:T(8,128)S(1)} all-to-all(f32[32,4,8,192]{3,0,1,2:T(8,128)S(1)} %copy.22), channel_id=1, replica_groups=mesh['wide'=8,'narrow'=4] {'wide'}, dimensions={2} | all-to-all | bytes 1572864 | tf_op jit(solution)/shard_map/all_to_all | solution.py:53
  213.7 0.1 copy.23
  213.8 15.7 %all-gather.2 = f32[32,1,1536]{0,1,2:T(1,128)S(1)} all-gather(f32[32,1,192]{0,1,2:T(1,128)S(1)} %copy.23), channel_id=4, replica_groups=mesh['wide'=8,'narrow'=4] {'wide'}, dimensions={2}, use_global_device_ids=true | all-gather | bytes 221184 | tf_op jit(solution)/shard_map/all_gather | solution.py:26
  229.6 2.6 fusion.21
  232.2 5.0 %fusion.10 = f32[32,3,1536]{2,0,1:T(8,128)} fusion(f32[6,192,1536]{2,1,0:T(8,128)} %param.8, f32[32,192]{1,0:T(8,128)S(1)} %fusion.21), kind=kOutput, calls=%fused_computation.12 | convolution fusion | flops 339738624 | bytes 4153344 | tf_op jit(solution)/shard_map/ks,qsc->kqc/dot_general | solution.py:32
  237.3 2.6 copy.28
  239.9 2.2 reshape.34
  242.2 29.2 %reduce-scatter.10.cloned.1.call-done = f32[192,96]{1,0:T(8,128)} async-done(((f32[1536,96]{1,0:T(8,128)}), f32[192,96]{1,0:T(8,128)}) %reduce-scatter.10.cloned.1.call-update) | async-done | bytes 73744
  271.4 1.1 reshape.35
  272.5 0.2 fusion.39
  272.7 0.1 copy.35
  272.8 0.1 copy.24
  272.9 16.0 %all-gather.3 = f32[32,1,1536]{0,1,2:T(1,128)S(1)} all-gather(f32[32,1,192]{0,1,2:T(1,128)S(1)} %copy.24), channel_id=5, replica_groups=mesh['wide'=8,'narrow'=4] {'wide'}, dimensions={2}, use_global_device_ids=true | all-gather | bytes 221184 | tf_op jit(solution)/shard_map/all_gather | solution.py:26
  288.9 2.6 fusion.19
  291.5 3.2 fusion.12
  294.7 0.8 copy.30
  295.5 1.8 reshape.36
  297.4 0.1 copy.37
  297.4 30.3 %reduce-scatter.12.cloned.1.call-done = f32[192,64]{1,0:T(8,128)} async-done(((f32[1536,64]{1,0:T(8,128)}), f32[192,64]{1,0:T(8,128)}) %reduce-scatter.12.cloned.1.call-update) | async-done | bytes 49168
  327.8 1.0 reshape.37
  328.8 0.2 fusion.40
  329.1 0.1 copy.25
  329.2 15.7 %all-gather.4 = f32[32,1,1536]{0,1,2:T(1,128)S(1)} all-gather(f32[32,1,192]{0,1,2:T(1,128)S(1)} %copy.25), channel_id=6, replica_groups=mesh['wide'=8,'narrow'=4] {'wide'}, dimensions={2}, use_global_device_ids=true | all-gather | bytes 221184 | tf_op jit(solution)/shard_map/all_gather | solution.py:26
  344.9 2.6 fusion.17
  347.5 4.8 %convolution_bitcast_fusion = f32[1536,32]{1,0:T(8,128)} fusion(f32[32,192]{1,0:T(8,128)S(1)} %fusion.17, f32[6,192,1536]{2,1,0:T(8,128)} %param.8), kind=kOutput, calls=%fused_computation.14 | convolution fusion | flops 113246208 | bytes 1400832 | tf_op jit(solution)/shard_map/ks,qsc->kqc/dot_general | solution.py:32
  352.3 0.1 copy.34
  352.4 0.1 copy.36
  352.5 30.3 %reduce-scatter.14.cloned.1.call-done = f32[192,32]{1,0:T(8,128)} async-done(((f32[1536,32]{1,0:T(8,128)}), f32[192,32]{1,0:T(8,128)}) %reduce-scatter.14.cloned.1.call-update) | async-done | bytes 24592
  382.8 1.0 copy.33
  383.8 0.1 copy.26
  383.9 15.7 %all-gather.5 = f32[32,1,1536]{0,1,2:T(1,128)S(1)} all-gather(f32[32,1,192]{0,1,2:T(1,128)S(1)} %copy.26), channel_id=7, replica_groups=mesh['wide'=8,'narrow'=4] {'wide'}, dimensions={2}, use_global_device_ids=true | all-gather | bytes 221184 | tf_op jit(solution)/shard_map/all_gather | solution.py:26
  399.6 2.6 fusion.28
  402.3 0.7 copy.27
  (21 shorter events, 0.4 us)
Async XLA Ops:
  7.2 264.3 %reduce-scatter.10.cloned.1.call-start = ((), (), s32[]{:S(2)}) async-start(), calls=%async_computation.6 | async-start | bytes 884736
  94.0 11.5 %copy-start = (f32[4,4,8,4096]{3,2,0,1:T(8,128)}, f32[4,4,8,4096]{3,2,0,1:T(8,128)S(1)}, u32[]{:S(2)}) copy-start(f32[4,4,8,4096]{3,2,0,1:T(8,128)S(1)} %copy.39) | copy-start | bytes 6291460
  94.0 25.8 %copy-start.2 = (f32[2,256,256]{2,1,0:T(8,128)S(1)}, f32[2,256,256]{2,1,0:T(8,128)}, u32[]{:S(2)}) copy-start(f32[2,256,256]{2,1,0:T(8,128)} %param.7) | copy-start | bytes 1572868
  181.5 1.3 copy-start.1
  242.1 85.6 %reduce-scatter.12.cloned.1.call-start = ((), (), s32[]{:S(2)}) async-start(), calls=%async_computation.7 | async-start | bytes 884736
  297.3 85.5 %reduce-scatter.14.cloned.1.call-start = ((), (), s32[]{:S(2)}) async-start(), calls=%async_computation.8 | async-start | bytes 884736
Sparse Core Ops, SparseCore 0:
  242.3 29.1 reduce-scatter.9
  297.4 30.2 reduce-scatter.11
  352.5 30.2 reduce-scatter.13
